TPU v7x, 32 devices: a whole 2x2x4 slice. The times are simulated.
32 devices in a mesh: dp: 8 (over z, y), mp: 4 (over x, core).
Axes of the slice: x: 2, y: 2, z: 4, core: 2. Of those that a mesh axis runs over, the one named last changes fastest.
Arguments:
- pred_input: bfloat16 [512, 256, 384], P('dp'), may hold values from -6 to 6
- proj_weight: bfloat16 [384, 1280], P('dp', 'mp'), may hold values from -0.3125 to 0.3125
- proj_bias: float32 [1280], P('mp'), may hold values from -3 to 3
- targets: bfloat16 [512, 256, 1280], P('dp', None, 'mp'), may hold values from -6 to 6
- block_masks: int32 [512, 4, 256], P('dp'), may hold values from 0 to 1, as said below
Outputs:
- loss: float32 [], replicated
- clip_scale: float32 [], replicated
- grad_weight: float32 [384, 1280], P('dp', 'mp')
- grad_bias: float32 [1280], P('mp')
Inputs may be any that keep to these rules, and one draw needn't show every extreme that they name: `block_masks`: each of an image's 4 target blocks is a nonempty rectangle of patches on the 16 x 16 grid (row-major patch order); blocks may intersect.
All inputs are finite; a program needn't handle non-finite values.
Results may differ from a plain program's by a relative error of at most 0.0003.
Values may be sent and summed in bfloat16 or wider, within the bound.
A program may use at most 192 MiB of HBM per device.

v0:
```python
import jax
import jax.numpy as jnp
from jax import lax
from jax.sharding import PartitionSpec as P


def body(pred_input, proj_weight, proj_bias, targets, block_masks):
    images_here, patches, pred_width = pred_input.shape
    feat_local = targets.shape[2]
    feat_full = feat_local * lax.axis_size("mp")
    token_count = images_here * patches
    coverage = jnp.sum(block_masks, axis=1).astype(jnp.float32)
    share = patches // lax.axis_size("mp")
    owned_cover = lax.dynamic_slice_in_dim(coverage, lax.axis_index("mp") * share, share, 1)
    count_part = jnp.sum(owned_cover)
    target_f = targets.astype(jnp.float32).reshape(token_count, feat_local)
    feat_sums, feat_squares = lax.psum(
        (jnp.sum(target_f, axis=1), jnp.sum(target_f * target_f, axis=1)), "mp"
    )
    mean_feat = feat_sums / feat_full
    variance = feat_squares / feat_full - mean_feat * mean_feat
    tnorm = (target_f - mean_feat[:, None]) * lax.rsqrt(variance[:, None] + 1e-05)
    inputs_flat = pred_input.reshape(token_count, pred_width)
    weight_full = lax.all_gather(proj_weight, "dp", axis=0, tiled=True)
    pred = jnp.dot(inputs_flat, weight_full, preferred_element_type=jnp.float32) + proj_bias
    differ = pred - tnorm
    magnitude = jnp.abs(differ)
    smooth = jnp.where(magnitude < 1.0, 0.5 * differ * differ, magnitude - 0.5)
    cover_column = coverage.reshape(token_count, 1)
    loss_part = jnp.sum(cover_column * smooth)
    clipped = cover_column * jnp.clip(differ, -1.0, 1.0)
    source = clipped.astype(jnp.bfloat16)
    grad_full = lax.dot_general(
        inputs_flat, source, (((0,), (0,)), ((), ())), preferred_element_type=jnp.float32
    )
    bias_part = jnp.sum(clipped, axis=0)
    grad_rows = lax.psum_scatter(grad_full, "dp", scatter_dimension=0, tiled=True)
    bias_grad = lax.psum(bias_part, "dp")
    bias_square = jnp.where(lax.axis_index("dp") == 0, jnp.sum(bias_grad * bias_grad), 0.0)
    square_part = jnp.sum(grad_rows * grad_rows) + bias_square
    total = lax.psum(count_part, ("dp", "mp"))
    loss_total = lax.psum(loss_part, ("dp", "mp"))
    square_total = lax.psum(square_part, ("dp", "mp"))
    norm = jnp.sqrt(square_total) / total
    clip_scale = jnp.minimum(1.0, 1.0 / (norm + 1e-06))
    factor = clip_scale / total
    loss = loss_total / total / feat_full
    return (loss, clip_scale, grad_rows * factor, bias_grad * factor)


def solution(mesh):
    in_specs = (
        P("dp", None, None),
        P("dp", "mp"),
        P("mp"),
        P("dp", None, "mp"),
        P("dp", None, None),
    )
    out_specs = (P(), P(), P("dp", "mp"), P("mp"))
    return jax.shard_map(body, mesh=mesh, in_specs=in_specs, out_specs=out_specs, check_vma=False)
```

profile of v0, /device:TPU:0, one launch (start us, length us, event | category | flops | bytes accessed | tf_op | source)
XLA Modules:
  0.0 243.8 jit_solution(10438953832590673611)
XLA Ops:
  7.2 0.0 all-reduce.4.cloned.1.call-start
  7.2 9.9 %convert_reduce_fusion = (f32[64,256]{1,0:T(8,128)S(1)}, f32[64,256]{1,0:T(8,128)S(1)}) fusion(bf16[64,256,320]{1,2,0:T(8,128)(2,1)} %param.8), kind=kLoop, calls=%fused_computation.2 | loop fusion | flops 20938752 | bytes 10616832 | tf_op jit(solution)/shard_map/reduce_sum | solution.py:18
  17.2 0.7 copy.19
  17.8 0.7 copy.20
  18.5 0.0 all-reduce.4.cloned.1.call-update
  18.5 0.0 reduce-scatter.4.cloned.1.call-start
  18.5 13.9 %convert_bitcast_fusion = f32[64,40,8,256]{3,2,1,0:T(8,128)} fusion(bf16[64,256,320]{1,2,0:T(8,128)(2,1)} %param.8), kind=kLoop, calls=%fused_computation.3 | loop fusion | flops 5242880 | bytes 31457280
  32.4 0.2 reduce_sum.76
  32.7 15.9 %copy.17 = f32[64,40,8,256]{3,2,0,1:T(8,128)} copy(f32[64,40,8,256]{3,2,1,0:T(8,128)} %convert_bitcast_fusion) | data formatting | bytes 41943040 | tf_op jit(solution)/shard_map/reshape | solution.py:16
  48.6 32.7 %all_gather.3 = bf16[384,320]{1,0:T(8,128)(2,1)S(1)} all-gather(bf16[48,320]{1,0:T(8,128)(2,1)S(1)} %copy-done.1), channel_id=1, replica_groups=mesh['dp'=8,'mp'=4] {'dp'}, dimensions={0}, use_global_device_ids=true | all-gather | bytes 276480 | tf_op jit(solution)/shard_map/all_gather | solution.py:24
  81.3 0.9 broadcast_multiply_fusion.1
  82.2 26.1 %fusion.5 = (f32[320]{0:T(512)S(1)}, f32[]{:T(128)}, f32[16384,320]{0,1:T(8,128)}) fusion(f32[16384]{0:T(1024)S(1)} %bitcast.20, f32[16384]{0:T(1024)S(1)} %get-tuple-element.28, f32[16384,320]{0,1:T(8,128)} %bitcast.19, f32[16384]{0:T(1024)S(1)} %get-tuple-element.27, f32[320]{0:T(512)S(1)} %copy-done.2, bf16[16384,384]{1,0:T(8,128)(2,1)} %bitcast.17, ...), kind=kOutput, calls=%fused_computation.11 | convolution fusion | flops 4105174784 | bytes 54970884 | tf_op jit(solution)/shard_map/dot_general | solution.py:25
  108.3 13.5 %fusion.12 = f32[384,320]{0,1:T(8,128)S(1)} fusion(bf16[16384,384]{1,0:T(8,128)(2,1)} %bitcast.18, f32[16384,320]{0,1:T(8,128)} %get-tuple-element.29, f32[16384]{0:T(1024)S(1)} %bitcast.21), kind=kOutput, calls=%fused_computation.17 | convolution fusion | flops 4042260480 | bytes 34111488 | tf_op jit(solution)/shard_map/dot_general | solution.py:33
  121.8 1.0 copy.15
  122.8 0.0 reduce-scatter.4.cloned.1.call-update
  122.9 0.7 dynamic-slice_reduce_fusion
  123.5 21.5 %psum.46 = f32[320]{0:T(512)S(1)} all-reduce(f32[320]{0:T(512)S(1)} %get-tuple-element.16), channel_id=1, replica_groups=mesh['dp'=8,'mp'=4] {'dp'}, use_global_device_ids=true, to_apply=%region_12.13 | all-reduce | flops 320 | bytes 2560 | tf_op jit(solution)/shard_map/psum | solution.py:38
  145.1 0.6 multiply_reduce_fusion.1
  146.3 40.9 %reduce-scatter.4.cloned.1.call-done = f32[48,320]{1,0:T(8,128)} async-done(((f32[384,320]{1,0:T(8,128)}), f32[48,320]{1,0:T(8,128)}) %reduce-scatter.4.cloned.1.call-update) | async-done | bytes 61456
  187.2 1.0 copy.16
  188.2 0.6 multiply_reduce_fusion
  189.5 40.3 %all-reduce = (f32[]{:T(128)}, f32[]{:T(128)}, f32[]{:T(128)}) all-reduce(f32[]{:T(128)} %get-tuple-element.17, f32[]{:T(128)} %dynamic-slice_reduce_fusion, f32[]{:T(128)S(6)} %add.44), channel_id=1, replica_groups=mesh['dp'=8,'mp'=4] {'dp','mp'}, use_global_device_ids=true, to_apply=%region_6.7 | all-reduce | flops 3 | bytes 24 | tf_op jit(solution)/shard_map/psum | solution.py:42
  232.0 0.6 broadcast_multiply_fusion.2
  233.9 0.7 copy.14
  (10 shorter events, 0.1 us)
Async XLA Ops:
  7.2 25.3 %copy-start = (s32[64,4,256]{2,1,0:T(4,128)S(1)}, s32[64,4,256]{2,1,0:T(4,128)}, u32[]{:S(2)}) copy-start(s32[64,4,256]{2,1,0:T(4,128)} %param.9) | copy-start | bytes 786436
  7.2 74.2 %all-reduce.4.cloned.1.call-start = ((), (), s32[]{:S(2)}) async-start(), calls=%async_computation.2 | async-start | bytes 262144 | tf_op jit(solution)/shard_map/psum | solution.py:17
  18.5 168.7 %reduce-scatter.4.cloned.1.call-start = ((), (), s32[]{:S(2)}) async-start(), calls=%async_computation.1 | async-start | bytes 663552
  32.7 16.0 %copy-start.1 = (bf16[48,320]{1,0:T(8,128)(2,1)S(1)}, bf16[48,320]{1,0:T(8,128)(2,1)}, u32[]{:S(2)}) copy-start(bf16[48,320]{1,0:T(8,128)(2,1)} %param.6) | copy-start | bytes 92164
  32.7 49.6 %copy-start.2 = (f32[320]{0:T(512)S(1)}, f32[320]{0:T(512)}, u32[]{:S(2)}) copy-start(f32[320]{0:T(512)} %param.7) | copy-start | bytes 3844
Sparse Core Ops, SparseCore 0:
  18.6 34.5 all-reduce.3
  123.0 64.2 reduce-scatter.3
where the time goes:
time: 244 us
  blocking collectives  94.6 us (39%)
  waiting for transfers between devices  41 us (17%)
  matrix products  39.5 us (16%)
  other arithmetic  27.4 us (11%)
  between operations  21.1 us (9%)
  local copies, waits for them, and re-layouts  20.1 us (8%)
    unnamed x3, waiting for transfers between devices  41 us
    psum x1, blocking collectives, body(): loss_total = lax.psum(loss_part, ('dp', 'mp'))  40.3 us
    all_gather x1, blocking collectives, body(): weight_full = lax.all_gather(proj_weight, 'dp', axis=0, tiled=True)  32.7 us
    dot_general x1, matrix products, body(): jnp.dot(inputs_flat, weight_full, preferred_element_type=jnp.float32)  26.1 us
    psum x1, blocking collectives, body(): bias_grad = lax.psum(bias_part, 'dp')  21.5 us
    reshape x1, local copies, waits for them, and re-layouts, body(): target_f = targets.astype(jnp.float32).reshape(token_count, feat_local)  15.9 us
    unnamed x1, other arithmetic  13.9 us
    dot_general x1, matrix products, body(): lax.dot_general(inputs_flat, source, (((0,), (0,)), ((), ())), preferred_...  13.5 us
  transfers between devices with their start and end apart: 2, of which 1 were waited for; matrix products, arithmetic and copies ran while one was open for 13% of the time, Pallas kernels for 0%

commit v1 on v0

--- a/solution.py
+++ b/solution.py
@@ -21,7 +21,16 @@
     variance = feat_squares / feat_full - mean_feat * mean_feat
     tnorm = (target_f - mean_feat[:, None]) * lax.rsqrt(variance[:, None] + 1e-05)
     inputs_flat = pred_input.reshape(token_count, pred_width)
-    weight_full = lax.all_gather(proj_weight, "dp", axis=0, tiled=True)
+    count_all = lax.axis_size("dp")
+    wide_out = sorted(((dev_j, (dev_j + 1) % count_all) for dev_j in range(count_all)))
+    part_next = proj_weight
+    pages = [part_next]
+    for m in tuple(range(1, count_all)):
+        part_next = lax.ppermute(part_next, "dp", perm=wide_out)
+        pages.insert(0, part_next)
+    met_up = jnp.concatenate(pages, axis=0)
+    before = lax.axis_index("dp")
+    weight_full = jnp.roll(met_up, (before + 1) * proj_weight.shape[0], axis=0)
     pred = jnp.dot(inputs_flat, weight_full, preferred_element_type=jnp.float32) + proj_bias
     differ = pred - tnorm
     magnitude = jnp.abs(differ)

time: 244 us -> 238 us (0.975)
  blocking collectives: 94.6 us -> 59.8 us
  waiting for transfers between devices: 41 us -> 66.3 us
  starting transfers between devices: 0.08 us -> 4.18 us
    all_gather x1 -> x0, blocking collectives: 32.7 us -> none  [body(): weight_full = lax.all_gather(proj_weight, 'dp', axis=0, tiled=True)]
    ppermute x0 -> x7, waiting for transfers between devices: none -> 21 us  [body(): part_next = lax.ppermute(part_next, 'dp', perm=wide_out)]
    ppermute x0 -> x7, starting transfers between devices: none -> 4.1 us  [body(): part_next = lax.ppermute(part_next, 'dp', perm=wide_out)]
  transfers between devices with their start and end apart: 2 -> 9, of which waited for: 1 -> 6; matrix products, arithmetic and copies ran while one was open for 13% -> 18% of each run, Pallas kernels for 0% -> 0%
where the time goes in v1:
time: 238 us
  waiting for transfers between devices  66.3 us (28%)
  blocking collectives  59.8 us (25%)
  matrix products  38.7 us (16%)
  other arithmetic  27.3 us (11%)
  between operations  21.3 us (9%)
  local copies, waits for them, and re-layouts  20.2 us (8%)
  starting transfers between devices  4.18 us (2%)
    unnamed x3, waiting for transfers between devices  42.9 us
    psum x1, blocking collectives, body(): loss_total = lax.psum(loss_part, ('dp', 'mp'))  40.4 us
    dot_general x1, matrix products, body(): jnp.dot(inputs_flat, weight_full, preferred_element_type=jnp.float32)  25.3 us
    ppermute x7, waiting for transfers between devices, body(): part_next = lax.ppermute(part_next, 'dp', perm=wide_out)  21 us
    psum x1, blocking collectives, body(): bias_grad = lax.psum(bias_part, 'dp')  19.4 us
    reshape x1, local copies, waits for them, and re-layouts, body(): target_f = targets.astype(jnp.float32).reshape(token_count, feat_local)  15.9 us
    unnamed x1, other arithmetic  13.9 us
    dot_general x1, matrix products, body(): lax.dot_general(inputs_flat, source, (((0,), (0,)), ((), ())), preferred_...  13.5 us
  transfers between devices with their start and end apart: 9, of which 6 were waited for; matrix products, arithmetic and copies ran while one was open for 18% of the time, Pallas kernels for 0%

profile of v1, /device:TPU:0, one launch (start us, length us, event | category | flops | bytes accessed | tf_op | source)
XLA Modules:
  0.0 237.8 jit_solution(12005120705016040503)
XLA Ops:
  7.2 3.0 %collective-permute-start = (bf16[48,320]{1,0:T(8,128)(2,1)}, bf16[48,320]{1,0:T(8,128)(2,1)S(1)}, u32[]{:S(2)}, u32[]{:S(2)}) collective-permute-start(bf16[48,320]{1,0:T(8,128)(2,1)} %param.6), channel_id=1, source_target_pairs={{0,4},{4,8},{8,12},{12,16},{16,20},{20,24},{24,28},{28,0},{1,5},{5... | collective-permute-start | bytes 92168 | tf_op jit(solution)/shard_map/ppermute | solution.py:29
  10.3 5.2 %collective-permute-done = bf16[48,320]{1,0:T(8,128)(2,1)S(1)} collective-permute-done((bf16[48,320]{1,0:T(8,128)(2,1)}, bf16[48,320]{1,0:T(8,128)(2,1)S(1)}, u32[]{:S(2)}, u32[]{:S(2)}) %collective-permute-start) | collective-permute-done | bytes 30752 | tf_op jit(solution)/shard_map/ppermute | solution.py:29
  15.5 6.7 %collective-permute-done.1 = bf16[48,320]{1,0:T(8,128)(2,1)S(1)} collective-permute-done((bf16[48,320]{1,0:T(8,128)(2,1)S(1)}, bf16[48,320]{1,0:T(8,128)(2,1)S(1)}, u32[]{:S(2)}, u32[]{:S(2)}) %collective-permute-start.1) | collective-permute-done | bytes 30752 | tf_op jit(solution)/shard_map/ppermute | solution.py:29
  22.1 6.7 %collective-permute-done.2 = bf16[48,320]{1,0:T(8,128)(2,1)S(1)} collective-permute-done((bf16[48,320]{1,0:T(8,128)(2,1)S(1)}, bf16[48,320]{1,0:T(8,128)(2,1)S(1)}, u32[]{:S(2)}, u32[]{:S(2)}) %collective-permute-start.2) | collective-permute-done | bytes 30752 | tf_op jit(solution)/shard_map/ppermute | solution.py:29
  28.8 9.9 %convert_reduce_fusion = (f32[64,256]{1,0:T(8,128)S(1)}, f32[64,256]{1,0:T(8,128)S(1)}) fusion(bf16[64,256,320]{1,2,0:T(8,128)(2,1)} %param.8), kind=kLoop, calls=%fused_computation.2 | loop fusion | flops 20938752 | bytes 10616832 | tf_op jit(solution)/shard_map/reduce_sum | solution.py:18
  38.7 0.7 copy.19
  39.3 0.7 copy.20
  40.1 13.9 %convert_bitcast_fusion = f32[64,40,8,256]{3,2,1,0:T(8,128)} fusion(bf16[64,256,320]{1,2,0:T(8,128)(2,1)} %param.8), kind=kLoop, calls=%fused_computation.3 | loop fusion | flops 5242880 | bytes 31457280
  54.4 15.9 %copy.17 = f32[64,40,8,256]{3,2,0,1:T(8,128)} copy(f32[64,40,8,256]{3,2,1,0:T(8,128)} %convert_bitcast_fusion) | data formatting | bytes 41943040 | tf_op jit(solution)/shard_map/reshape | solution.py:16
  70.3 0.9 collective-permute-start.6
  71.2 2.4 all-reduce.4.cloned.1.call-done
  73.6 0.9 broadcast_multiply_fusion.1
  74.5 2.5 %collective-permute-done.6 = bf16[48,320]{1,0:T(8,128)(2,1)S(1)} collective-permute-done((bf16[48,320]{1,0:T(8,128)(2,1)S(1)}, bf16[48,320]{1,0:T(8,128)(2,1)S(1)}, u32[]{:S(2)}, u32[]{:S(2)}) %collective-permute-start.6) | collective-permute-done | bytes 30752 | tf_op jit(solution)/shard_map/ppermute | solution.py:29
  77.2 25.3 %fusion.6 = (f32[320]{0:T(512)S(1)}, f32[]{:T(128)}, f32[16384,320]{0,1:T(8,128)}) fusion(f32[16384]{0:T(1024)S(1)} %bitcast.23, f32[16384]{0:T(1024)S(1)} %get-tuple-element.28, f32[16384,320]{0,1:T(8,128)} %bitcast.22, f32[16384]{0:T(1024)S(1)} %get-tuple-element.27, f32[320]{0:T(512)S(1)} %copy-done.2, bf16[16384,384]{1,0:T(8,128)(2,1)} %bitcast.20, ...), kind=kOutput, calls=%fused_computation.12 | convolution fusion | flops 4105174784 | bytes 55020808 | tf_op jit(solution)/shard_map/dot_general | solution.py:34
  102.5 13.5 %fusion.13 = f32[384,320]{0,1:T(8,128)S(1)} fusion(bf16[16384,384]{1,0:T(8,128)(2,1)} %bitcast.21, f32[16384,320]{0,1:T(8,128)} %get-tuple-element.29, f32[16384]{0:T(1024)S(1)} %bitcast.24), kind=kOutput, calls=%fused_computation.18 | convolution fusion | flops 4042260480 | bytes 34111488 | tf_op jit(solution)/shard_map/dot_general | solution.py:42
  115.9 1.0 copy.15
  117.0 0.7 dynamic-slice_reduce_fusion
  117.7 19.4 %psum.46 = f32[320]{0:T(512)S(1)} all-reduce(f32[320]{0:T(512)S(1)} %get-tuple-element.16), channel_id=1, replica_groups=mesh['dp'=8,'mp'=4] {'dp'}, use_global_device_ids=true, to_apply=%region_12.13 | all-reduce | flops 320 | bytes 2560 | tf_op jit(solution)/shard_map/psum | solution.py:47
  137.1 0.6 multiply_reduce_fusion.1
  138.4 42.9 %reduce-scatter.4.cloned.1.call-done = f32[48,320]{1,0:T(8,128)} async-done(((f32[384,320]{1,0:T(8,128)}), f32[48,320]{1,0:T(8,128)}) %reduce-scatter.4.cloned.1.call-update) | async-done | bytes 61456
  181.3 1.0 copy.16
  182.3 0.6 multiply_reduce_fusion
  183.6 40.4 %all-reduce = (f32[]{:T(128)}, f32[]{:T(128)}, f32[]{:T(128)}) all-reduce(f32[]{:T(128)} %get-tuple-element.17, f32[]{:T(128)} %dynamic-slice_reduce_fusion, f32[]{:T(128)S(6)} %add.64), channel_id=1, replica_groups=mesh['dp'=8,'mp'=4] {'dp','mp'}, use_global_device_ids=true, to_apply=%region_6.7 | all-reduce | flops 3 | bytes 24 | tf_op jit(solution)/shard_map/psum | solution.py:51
  228.0 0.7 copy.14
  (39 shorter events, 1.2 us)
Async XLA Ops:
  7.2 46.8 %copy-start = (s32[64,4,256]{2,1,0:T(4,128)S(1)}, s32[64,4,256]{2,1,0:T(4,128)}, u32[]{:S(2)}) copy-start(s32[64,4,256]{2,1,0:T(4,128)} %param.9) | copy-start | bytes 786436
  7.2 66.4 %all-reduce.4.cloned.1.call-start = ((), (), s32[]{:S(2)}) async-start(), calls=%async_computation.2 | async-start | bytes 262144 | tf_op jit(solution)/shard_map/psum | solution.py:17
  7.2 8.2 %collective-permute-start = (bf16[48,320]{1,0:T(8,128)(2,1)}, bf16[48,320]{1,0:T(8,128)(2,1)S(1)}, u32[]{:S(2)}, u32[]{:S(2)}) collective-permute-start(bf16[48,320]{1,0:T(8,128)(2,1)} %param.6), channel_id=1, source_target_pairs={{0,4},{4,8},{8,12},{12,16},{16,20},{20,24},{24,28},{28,0},{1,5},{5... | collective-permute-start | bytes 92168 | tf_op jit(solution)/shard_map/ppermute | solution.py:29
  15.5 6.7 %collective-permute-start.1 = (bf16[48,320]{1,0:T(8,128)(2,1)S(1)}, bf16[48,320]{1,0:T(8,128)(2,1)S(1)}, u32[]{:S(2)}, u32[]{:S(2)}) collective-permute-start(bf16[48,320]{1,0:T(8,128)(2,1)S(1)} %collective-permute-done), channel_id=1, source_target_pairs={{0,4},{4,8},{8,12},{12,16},{16,20},{20,24},{24,28},{28,0},{1,5},{5... | collective-permute-start | bytes 92168 | tf_op jit(solution)/shard_map/ppermute | solution.py:29
  22.1 6.7 %collective-permute-start.2 = (bf16[48,320]{1,0:T(8,128)(2,1)S(1)}, bf16[48,320]{1,0:T(8,128)(2,1)S(1)}, u32[]{:S(2)}, u32[]{:S(2)}) collective-permute-start(bf16[48,320]{1,0:T(8,128)(2,1)S(1)} %collective-permute-done.1), channel_id=1, source_target_pairs={{0,4},{4,8},{8,12},{12,16},{16,20},{20,24},{24,28},{28,0},{1,5},{5... | collective-permute-start | bytes 92168 | tf_op jit(solution)/shard_map/ppermute | solution.py:29
  28.8 11.3 %collective-permute-start.3 = (bf16[48,320]{1,0:T(8,128)(2,1)S(1)}, bf16[48,320]{1,0:T(8,128)(2,1)S(1)}, u32[]{:S(2)}, u32[]{:S(2)}) collective-permute-start(bf16[48,320]{1,0:T(8,128)(2,1)S(1)} %collective-permute-done.2), channel_id=1, source_target_pairs={{0,4},{4,8},{8,12},{12,16},{16,20},{20,24},{24,28},{28,0},{1,5},{5... | collective-permute-start | bytes 92168 | tf_op jit(solution)/shard_map/ppermute | solution.py:29
  40.0 141.3 %reduce-scatter.4.cloned.1.call-start = ((), (), s32[]{:S(2)}) async-start(), calls=%async_computation.1 | async-start | bytes 663552
  40.1 14.1 %collective-permute-start.4 = (bf16[48,320]{1,0:T(8,128)(2,1)S(1)}, bf16[48,320]{1,0:T(8,128)(2,1)S(1)}, u32[]{:S(2)}, u32[]{:S(2)}) collective-permute-start(bf16[48,320]{1,0:T(8,128)(2,1)S(1)} %collective-permute-done.3), channel_id=1, source_target_pairs={{0,4},{4,8},{8,12},{12,16},{16,20},{20,24},{24,28},{28,0},{1,5},{5... | collective-permute-start | bytes 92168 | tf_op jit(solution)/shard_map/ppermute | solution.py:29
  54.2 16.1 %collective-permute-start.5 = (bf16[48,320]{1,0:T(8,128)(2,1)S(1)}, bf16[48,320]{1,0:T(8,128)(2,1)S(1)}, u32[]{:S(2)}, u32[]{:S(2)}) collective-permute-start(bf16[48,320]{1,0:T(8,128)(2,1)S(1)} %collective-permute-done.4), channel_id=1, source_target_pairs={{0,4},{4,8},{8,12},{12,16},{16,20},{20,24},{24,28},{28,0},{1,5},{5... | collective-permute-start | bytes 92168 | tf_op jit(solution)/shard_map/ppermute | solution.py:29
  54.3 22.7 %copy-start.1 = (bf16[48,320]{1,0:T(8,128)(2,1)S(1)}, bf16[48,320]{1,0:T(8,128)(2,1)}, u32[]{:S(2)}) copy-start(bf16[48,320]{1,0:T(8,128)(2,1)} %param.6) | copy-start | bytes 92164
  54.3 22.8 %copy-start.2 = (f32[320]{0:T(512)S(1)}, f32[320]{0:T(512)}, u32[]{:S(2)}) copy-start(f32[320]{0:T(512)} %param.7) | copy-start | bytes 3844
  70.3 6.7 %collective-permute-start.6 = (bf16[48,320]{1,0:T(8,128)(2,1)S(1)}, bf16[48,320]{1,0:T(8,128)(2,1)S(1)}, u32[]{:S(2)}, u32[]{:S(2)}) collective-permute-start(bf16[48,320]{1,0:T(8,128)(2,1)S(1)} %collective-permute-done.5), channel_id=1, source_target_pairs={{0,4},{4,8},{8,12},{12,16},{16,20},{20,24},{24,28},{28,0},{1,5},{5... | collective-permute-start | bytes 92168 | tf_op jit(solution)/shard_map/ppermute | solution.py:29
Sparse Core Ops, SparseCore 0:
  40.1 33.3 all-reduce.3
  117.1 64.1 reduce-scatter.3
